TPU v7x, 32 devices: a whole 2x2x4 slice. The times are simulated.
32 devices in a mesh: outer: 4 (over z), inner: 8 (over y, x, core).
Axes of the slice: x: 2, y: 2, z: 4, core: 2. Of those that a mesh axis runs over, the one named last changes fastest.
Arguments:
- query_proj: bfloat16 [2048, 8192], P(('outer', 'inner')), may hold values from -8 to 8
- key_proj: bfloat16 [2048, 512], P(('outer', 'inner')), may hold values from -8 to 8
- value_proj: bfloat16 [2048, 512], P(('outer', 'inner')), may hold values from -6 to 6
- positions: int32 [2048], P(('outer', 'inner')), may hold values from 0 to 2047, each once
Outputs:
- attended: bfloat16 [2048, 8192], P(('outer', 'inner'))
Inputs may be any that keep to these rules, and one draw needn't show every extreme that they name: `positions`: each position from 0 to 2047 appears exactly once.
All inputs are finite; a program needn't handle non-finite values.
Results may differ from a plain program's by a relative error of at most 0.005.
Values may be sent and summed in bfloat16 or wider, within the bound.
A program may use at most 64 MiB of HBM per device.

v0:
```python
import math
import jax
import jax.numpy as jnp
from jax import lax
from jax.sharding import PartitionSpec as P

HEAD_WIDTH = 128
masked_score = -1e30


def update(carried, key_value_block, key_pos, query_cluster, query_pos):
    running_top, running_sum, accumulated = carried
    heads_kv = query_cluster.shape[0]
    head_dim = query_cluster.shape[2]
    width = heads_kv * head_dim
    rows_kv = key_value_block.shape[0]
    key_slice = key_value_block[:, :width].reshape(rows_kv, heads_kv, head_dim)
    value_slice = key_value_block[:, width:].reshape(rows_kv, heads_kv, head_dim)
    scores = jnp.einsum(
        "lva,vga->vlg", key_slice, query_cluster, preferred_element_type=jnp.float32
    ) * (1.0 / math.sqrt(head_dim))
    visible = key_pos[None, :, None] <= query_pos[None, None, :]
    block_top = jnp.max(jnp.where(visible, scores, masked_score), axis=1)
    new_top = jnp.maximum(running_top, block_top)
    softmax_weights = jnp.where(visible, jnp.exp(scores - new_top[:, None, :]), 0.0)
    rescale = jnp.exp(running_top - new_top)
    running_sum = running_sum * rescale + jnp.sum(softmax_weights, axis=1)
    accumulated = accumulated * rescale[:, :, None] + jnp.einsum(
        "goi,ogt->git",
        softmax_weights.astype(jnp.bfloat16),
        value_slice,
        preferred_element_type=jnp.float32,
    )
    return (new_top, running_sum, accumulated)


def make_folder(query_cluster, query_pos):

    def fold_piece(carried, kv_piece, first_row):
        kv_rows, key_pos = kv_piece
        row_count = kv_rows.shape[0]
        sub_rows = math.gcd(row_count, 512)
        stacked = kv_rows.reshape(row_count // sub_rows, sub_rows, kv_rows.shape[1])
        pos_stack = key_pos.reshape(row_count // sub_rows, sub_rows)

        def inner_step(carry_in, sub_block):
            return (update(carry_in, sub_block[0], sub_block[1], query_cluster, query_pos), None)

        carried, unused = lax.scan(inner_step, carried, (stacked, pos_stack))
        return carried

    return fold_piece


def start_state(heads_kv, query_rows, head_dim):
    return (
        jnp.full((heads_kv, query_rows), masked_score, jnp.float32),
        jnp.zeros((heads_kv, query_rows), jnp.float32),
        jnp.zeros((heads_kv, query_rows, head_dim), jnp.float32),
    )


def finish(carried):
    return carried[2] / carried[1][:, :, None]


def body(query_proj, key_proj, value_proj, positions):
    tok_rows = query_proj.shape[0]
    head_dim = HEAD_WIDTH
    heads_all = query_proj.shape[1] // head_dim
    heads_kv = key_proj.shape[1] // head_dim
    group_size = heads_all // heads_kv
    inner_count = lax.axis_size("inner")
    per_device = heads_all // inner_count
    repeat_count = group_size // per_device
    key_spread = jnp.repeat(key_proj.reshape(tok_rows, heads_kv, head_dim), repeat_count, axis=1)
    value_broadcast = jnp.repeat(
        value_proj.reshape(tok_rows, heads_kv, head_dim), repeat_count, axis=1
    )
    kv_spread = jnp.concatenate([key_spread, value_broadcast], axis=2).reshape(
        tok_rows, inner_count * 2 * head_dim
    )
    query_heads, kv_heads = (
        lax.all_to_all(query_proj, "inner", split_axis=1, concat_axis=0, tiled=True),
        lax.all_to_all(kv_spread, "inner", split_axis=1, concat_axis=0, tiled=True),
    )
    group_pos = lax.all_gather(positions, "inner", axis=0, tiled=True)
    group_rows = query_heads.shape[0]
    query_cluster = (
        query_heads.reshape(group_rows, per_device, head_dim)
        .transpose(1, 0, 2)
        .reshape(1, per_device * group_rows, head_dim)
    )
    query_pos = jnp.tile(group_pos, per_device)
    folder = make_folder(query_cluster, query_pos)
    initial = start_state(1, per_device * group_rows, head_dim)
    carried = folder(
        initial,
        (
            lax.all_gather(kv_heads, "outer", axis=0, tiled=True),
            lax.all_gather(group_pos, "outer", axis=0, tiled=True),
        ),
        jnp.int32(0),
    )
    result = (
        finish(carried)
        .reshape(per_device, group_rows, head_dim)
        .transpose(1, 0, 2)
        .reshape(group_rows, per_device * head_dim)
        .astype(jnp.bfloat16)
    )
    return lax.all_to_all(result, "inner", split_axis=0, concat_axis=1, tiled=True)


def solution(mesh):
    return jax.shard_map(
        body,
        mesh=mesh,
        in_specs=(
            P(("outer", "inner"), None),
            P(("outer", "inner"), None),
            P(("outer", "inner"), None),
            P(("outer", "inner")),
        ),
        out_specs=P(("outer", "inner"), None),
        check_vma=False,
    )
```

profile of v0, /device:TPU:0, one launch (start us, length us, event | category | flops | bytes accessed | tf_op | source)
XLA Modules:
  0.0 115.0 jit_solution(7399036608634765369)
XLA Ops:
  6.5 0.8 copy-done
  7.4 0.9 copy_bitcast_fusion.2
  8.3 12.0 %all_to_all.48 = bf16[64,8,256]{2,0,1:T(8,128)(2,1)} all-to-all(bf16[64,8,256]{2,0,1:T(8,128)(2,1)S(1)} %pad_maximum_fusion), channel_id=1, replica_groups=mesh['outer'=4,'inner'=8] {'inner'}, dimensions={1} | all-to-all | bytes 524288 | tf_op jit(solution)/shard_map/all_to_all | solution.py:85
  20.4 2.3 %copy.35 = bf16[8,8,8,1024]{3,2,0,1:T(8,128)(2,1)} copy(bf16[8,8,8,1024]{3,2,1,0:T(8,128)(2,1)} %bitcast.91) | data formatting | bytes 2097152 | tf_op jit(solution)/shard_map/all_to_all | solution.py:84
  22.7 3.6 %all-to-all-start.1 = ((bf16[64,8,1024]{2,0,1:T(8,128)(2,1)}), bf16[64,8,1024]{2,0,1:T(8,128)(2,1)S(1)}, u32[]{:S(2)}, u32[]{:S(2)}) async-start(bf16[64,8,1024]{2,0,1:T(8,128)(2,1)} %bitcast.56), calls=%async_computation.1 | async-start | bytes 2097152 | tf_op jit(solution)/shard_map/all_to_all | solution.py:84
  26.3 1.3 %dynamic-slice = u32[1]{0:T(128)} dynamic-slice(u32[32]{0:T(128)} %constant.26, u32[]{:T(128)S(6)} %add.9), dynamic_slice_sizes={1} | dynamic-slice | bytes 12
  28.3 0.9 dynamic-update-slice
  29.1 14.7 %all-reduce = s32[512]{0:T(512)S(1)} all-reduce(s32[512]{0:T(512)S(1)} %dynamic-update-slice), channel_id=1, replica_groups=mesh['outer'=4,'inner'=8] {'inner'}, use_global_device_ids=true, to_apply=%add | all-reduce | flops 512 | bytes 4096
  43.8 12.1 %all-gather = s32[4,1,512]{2,1,0:T(1,128)S(1)} all-gather(s32[1,1,512]{2,1,0:T(1,128)S(1)} %bitcast.102), channel_id=1, replica_groups=mesh['outer'=4,'inner'=8] {'outer'}, dimensions={0}, use_global_device_ids=true | all-gather | bytes 10240 | tf_op jit(solution)/shard_map/all_gather | solution.py:101
  55.9 0.3 copy.29
  56.4 31.0 %while.15 = (s32[]{:T(128)}, f32[1,4096]{1,0:T(1,128)S(1)}, f32[1,4096]{1,0:T(1,128)S(1)}, f32[1,4096,128]{2,1,0:T(8,128)S(1)}, s32[4,512]{1,0:T(4,128)S(1)}, /*...) while((s32[]{:T(128)}, f32[1,4096]{1,0:T(1,128)S(1)}, ...), condition=%wide.region_3.4_spmd.clone, body=%wide.region_0.3_spmd.clone.sunk | while | flops 1104695296 | bytes 31568000 | solution.py:49
  56.5 1.0 dynamic-slice_bitcast_fusion.2
  57.4 1.4 %fusion.31 = (f32[4096]{0:T(1024)S(1)}, f32[512,4096]{1,0:T(8,128)S(1)}) fusion(s32[4096]{0:T(1024)S(1)} %bitcast.86, s32[512]{0:T(512)S(1)} %bitcast.99, bf16[1,4096,128]{2,1,0:T(8,128)(2,1)S(1)} %get-tuple-element.183, bf16[512,256]{1,0:T(8,128)(2,1)S(1)} %dynamic-slice_bitcast_fusion.2), kind=kOutput, calls=%fused_computation.3.clone.1 | convolution fusion | flops 545255424 | bytes 9603072 | tf_op jit(solution)/shard_map/while/body/eval_jaxpr/lva,vga->vlg/dot_general | solution.py:19
  58.9 2.2 %fusion.33 = f32[4096]{0:T(1024)S(1)} fusion(f32[512,4096]{1,0:T(8,128)S(1)} %get-tuple-element.154, f32[4096]{0:T(1024)S(1)} %bitcast.79, s32[4096]{0:T(1024)S(1)} %bitcast.87, s32[512]{0:T(512)S(1)} %bitcast.100), kind=kLoop, calls=%fused_computation.5.clone.1 | loop fusion | flops 10481664 | bytes 8439808 | tf_op jit(solution)/shard_map/while/body/eval_jaxpr/reduce_sum | solution.py:27
  61.2 3.0 %fusion.35 = f32[1,4096,128]{2,1,0:T(8,128)S(1)} fusion(f32[512,4096]{1,0:T(8,128)S(1)} %get-tuple-element.154, f32[4096]{0:T(1024)S(1)} %bitcast.80, s32[4096]{0:T(1024)S(1)} %bitcast.88, s32[512]{0:T(512)S(1)} %bitcast.101, f32[1,4096,128]{2,1,0:T(8,128)S(1)} %get-tuple-element.170, f32[4096]{0:T(1024)S(1)} %bitcast.98, pred[]{:T(512)S(6)} %compare.3, ...), kind=kOutput, calls=%fused_computation.7.clone.1 | convolution fusion | flops 548929536 | bytes 12765185 | tf_op jit(solution)/shard_map/while/body/eval_jaxpr/goi,ogt->git/dot_general | solution.py:28
  64.2 1.0 dynamic-slice_bitcast_fusion.2
  65.2 1.4 %fusion.31 = (f32[4096]{0:T(1024)S(1)}, f32[512,4096]{1,0:T(8,128)S(1)}) fusion(s32[4096]{0:T(1024)S(1)} %bitcast.86, s32[512]{0:T(512)S(1)} %bitcast.99, bf16[1,4096,128]{2,1,0:T(8,128)(2,1)S(1)} %get-tuple-element.183, bf16[512,256]{1,0:T(8,128)(2,1)S(1)} %dynamic-slice_bitcast_fusion.2), kind=kOutput, calls=%fused_computation.3.clone.1 | convolution fusion | flops 545255424 | bytes 9603072 | tf_op jit(solution)/shard_map/while/body/eval_jaxpr/lva,vga->vlg/dot_general | solution.py:19
  66.6 2.2 %fusion.33 = f32[4096]{0:T(1024)S(1)} fusion(f32[512,4096]{1,0:T(8,128)S(1)} %get-tuple-element.154, f32[4096]{0:T(1024)S(1)} %bitcast.79, s32[4096]{0:T(1024)S(1)} %bitcast.87, s32[512]{0:T(512)S(1)} %bitcast.100), kind=kLoop, calls=%fused_computation.5.clone.1 | loop fusion | flops 10481664 | bytes 8439808 | tf_op jit(solution)/shard_map/while/body/eval_jaxpr/reduce_sum | solution.py:27
  68.9 3.0 %fusion.35 = f32[1,4096,128]{2,1,0:T(8,128)S(1)} fusion(f32[512,4096]{1,0:T(8,128)S(1)} %get-tuple-element.154, f32[4096]{0:T(1024)S(1)} %bitcast.80, s32[4096]{0:T(1024)S(1)} %bitcast.88, s32[512]{0:T(512)S(1)} %bitcast.101, f32[1,4096,128]{2,1,0:T(8,128)S(1)} %get-tuple-element.170, f32[4096]{0:T(1024)S(1)} %bitcast.98, pred[]{:T(512)S(6)} %compare.3, ...), kind=kOutput, calls=%fused_computation.7.clone.1 | convolution fusion | flops 548929536 | bytes 12765185 | tf_op jit(solution)/shard_map/while/body/eval_jaxpr/goi,ogt->git/dot_general | solution.py:28
  71.9 1.0 dynamic-slice_bitcast_fusion.2
  72.9 1.4 %fusion.31 = (f32[4096]{0:T(1024)S(1)}, f32[512,4096]{1,0:T(8,128)S(1)}) fusion(s32[4096]{0:T(1024)S(1)} %bitcast.86, s32[512]{0:T(512)S(1)} %bitcast.99, bf16[1,4096,128]{2,1,0:T(8,128)(2,1)S(1)} %get-tuple-element.183, bf16[512,256]{1,0:T(8,128)(2,1)S(1)} %dynamic-slice_bitcast_fusion.2), kind=kOutput, calls=%fused_computation.3.clone.1 | convolution fusion | flops 545255424 | bytes 9603072 | tf_op jit(solution)/shard_map/while/body/eval_jaxpr/lva,vga->vlg/dot_general | solution.py:19
  74.4 2.2 %fusion.33 = f32[4096]{0:T(1024)S(1)} fusion(f32[512,4096]{1,0:T(8,128)S(1)} %get-tuple-element.154, f32[4096]{0:T(1024)S(1)} %bitcast.79, s32[4096]{0:T(1024)S(1)} %bitcast.87, s32[512]{0:T(512)S(1)} %bitcast.100), kind=kLoop, calls=%fused_computation.5.clone.1 | loop fusion | flops 10481664 | bytes 8439808 | tf_op jit(solution)/shard_map/while/body/eval_jaxpr/reduce_sum | solution.py:27
  76.7 3.0 %fusion.35 = f32[1,4096,128]{2,1,0:T(8,128)S(1)} fusion(f32[512,4096]{1,0:T(8,128)S(1)} %get-tuple-element.154, f32[4096]{0:T(1024)S(1)} %bitcast.80, s32[4096]{0:T(1024)S(1)} %bitcast.88, s32[512]{0:T(512)S(1)} %bitcast.101, f32[1,4096,128]{2,1,0:T(8,128)S(1)} %get-tuple-element.170, f32[4096]{0:T(1024)S(1)} %bitcast.98, pred[]{:T(512)S(6)} %compare.3, ...), kind=kOutput, calls=%fused_computation.7.clone.1 | convolution fusion | flops 548929536 | bytes 12765185 | tf_op jit(solution)/shard_map/while/body/eval_jaxpr/goi,ogt->git/dot_general | solution.py:28
  79.7 1.0 dynamic-slice_bitcast_fusion.2
  80.7 1.4 %fusion.31 = (f32[4096]{0:T(1024)S(1)}, f32[512,4096]{1,0:T(8,128)S(1)}) fusion(s32[4096]{0:T(1024)S(1)} %bitcast.86, s32[512]{0:T(512)S(1)} %bitcast.99, bf16[1,4096,128]{2,1,0:T(8,128)(2,1)S(1)} %get-tuple-element.183, bf16[512,256]{1,0:T(8,128)(2,1)S(1)} %dynamic-slice_bitcast_fusion.2), kind=kOutput, calls=%fused_computation.3.clone.1 | convolution fusion | flops 545255424 | bytes 9603072 | tf_op jit(solution)/shard_map/while/body/eval_jaxpr/lva,vga->vlg/dot_general | solution.py:19
  82.1 2.2 %fusion.33 = f32[4096]{0:T(1024)S(1)} fusion(f32[512,4096]{1,0:T(8,128)S(1)} %get-tuple-element.154, f32[4096]{0:T(1024)S(1)} %bitcast.79, s32[4096]{0:T(1024)S(1)} %bitcast.87, s32[512]{0:T(512)S(1)} %bitcast.100), kind=kLoop, calls=%fused_computation.5.clone.1 | loop fusion | flops 10481664 | bytes 8439808 | tf_op jit(solution)/shard_map/while/body/eval_jaxpr/reduce_sum | solution.py:27
  84.4 3.0 %fusion.35 = f32[1,4096,128]{2,1,0:T(8,128)S(1)} fusion(f32[512,4096]{1,0:T(8,128)S(1)} %get-tuple-element.154, f32[4096]{0:T(1024)S(1)} %bitcast.80, s32[4096]{0:T(1024)S(1)} %bitcast.88, s32[512]{0:T(512)S(1)} %bitcast.101, f32[1,4096,128]{2,1,0:T(8,128)S(1)} %get-tuple-element.170, f32[4096]{0:T(1024)S(1)} %bitcast.98, pred[]{:T(512)S(6)} %compare.3, ...), kind=kOutput, calls=%fused_computation.7.clone.1 | convolution fusion | flops 548929536 | bytes 12765185 | tf_op jit(solution)/shard_map/while/body/eval_jaxpr/goi,ogt->git/dot_general | solution.py:28
  87.4 0.7 divide_convert_fusion
  88.1 0.7 copy.36
  88.8 0.5 convert_element_type.20
  89.3 17.8 %all_to_all.49 = bf16[8,64,1024]{2,1,0:T(8,128)(2,1)S(1)} all-to-all(bf16[8,64,1024]{2,1,0:T(8,128)(2,1)S(1)} %convert_element_type.20), channel_id=1, replica_groups=mesh['outer'=4,'inner'=8] {'inner'}, dimensions={0} | all-to-all | bytes 2097152 | tf_op jit(solution)/shard_map/all_to_all | solution.py:112
  107.1 1.1 copy.28
  (39 shorter events, 0.7 us)
Async XLA Ops:
  6.5 0.8 copy-start
  6.5 49.9 %all-gather.3.cloned.1.call-start = ((), (), s32[]{:S(2)}) async-start(), calls=%async_computation.3 | async-start | bytes 1310720 | tf_op jit(solution)/shard_map/all_gather | solution.py:100
  22.7 33.3 %all-to-all-start.1 = ((bf16[64,8,1024]{2,0,1:T(8,128)(2,1)}), bf16[64,8,1024]{2,0,1:T(8,128)(2,1)S(1)}, u32[]{:S(2)}, u32[]{:S(2)}) async-start(bf16[64,8,1024]{2,0,1:T(8,128)(2,1)} %bitcast.56), calls=%async_computation.1 | async-start | bytes 2097152 | tf_op jit(solution)/shard_map/all_to_all | solution.py:84
Sparse Core Ops, SparseCore 0:
  20.5 27.3 all-gather.2
where the time goes:
time: 116 us; the launch traced here: 115 us
  blocking collectives  56.6 us (49%)
  matrix products  17.6 us (15%)
  between operations  14.2 us (12%)
  local copies, waits for them, and re-layouts  12.8 us (11%)
  other arithmetic  9.87 us (9%)
  starting transfers between devices  3.56 us (3%)
    all_to_all x1, blocking collectives, body(): lax.all_to_all(result, 'inner', split_axis=0, concat_axis=1, tiled=True)  17.8 us
    unnamed x1, blocking collectives  14.7 us
    all_gather x1, blocking collectives, body(): lax.all_gather(group_pos, 'outer', axis=0, tiled=True)  12.1 us
    all_to_all x1, blocking collectives, body(): lax.all_to_all(kv_spread, 'inner', split_axis=1, concat_axis=0, tiled=True)  12 us
    dot_general x4, matrix products, update(): jnp.einsum('goi,ogt->git', softmax_weights.astype(jnp.bfloat16), value_sl...  11.9 us
    reduce_sum x4, other arithmetic, update(): running_sum = running_sum * rescale + jnp.sum(softmax_weights, axis=1)  8.73 us
    dot_general x4, matrix products, update(): jnp.einsum('lva,vga->vlg', key_slice, query_cluster, preferred_element_ty...  5.72 us
    squeeze x4, local copies, waits for them, and re-layouts, fold_piece(): carried, unused = lax.scan(inner_step, carried, (stacked, pos_stack))  3.9 us
  transfers between devices with their start and end apart: 2, of which 0 were waited for; matrix products, arithmetic and copies ran while one was open for 4% of the time, Pallas kernels for 0%

commit v1 on v0

--- a/solution.py
+++ b/solution.py
@@ -1,11 +1,26 @@
+import functools
 import math
 import jax
 import jax.numpy as jnp
 from jax import lax
 from jax.sharding import PartitionSpec as P
+from jax.lax import all_to_all, axis_size
 
 HEAD_WIDTH = 128
 masked_score = -1e30
+
+
+def keep_up_sources_all(original, join_dim, pos_dim):
+    base_arr = jnp.concatenate(
+        all_to_all(
+            jnp.stack(jnp.split(original, axis_size("inner"), axis=join_dim), axis=0), "inner", 0, 0
+        ),
+        axis=pos_dim,
+    )
+    return base_arr
+
+
+supply_all_counts = functools.partial(keep_up_sources_all, join_dim=1, pos_dim=0)
 
 
 def update(carried, key_value_block, key_pos, query_cluster, query_pos):
@@ -81,7 +96,7 @@
         tok_rows, inner_count * 2 * head_dim
     )
     query_heads, kv_heads = (
-        lax.all_to_all(query_proj, "inner", split_axis=1, concat_axis=0, tiled=True),
+        supply_all_counts(query_proj),
         lax.all_to_all(kv_spread, "inner", split_axis=1, concat_axis=0, tiled=True),
     )
     group_pos = lax.all_gather(positions, "inner", axis=0, tiled=True)

time: 116 us -> 121 us (1.043)
  blocking collectives: 56.6 us -> 44.7 us
  local copies, waits for them, and re-layouts: 12.8 us -> 23.8 us
  starting transfers between devices: 3.56 us -> 9.39 us
    all_to_all x1 -> x0, blocking collectives: 12 us -> none  [body(): lax.all_to_all(kv_spread, 'inner', split_axis=1, concat_axis=0, tiled=True)]
    unnamed x7 -> x16, local copies, waits for them, and re-layouts: 3.28 us -> 15 us
    all_to_all x1 -> x2, starting transfers between devices: 3.56 us -> 9.35 us  [the longest x1 5.2 us: body(): lax.all_to_all(kv_spread, 'inner', split_axis=1, concat_axis=0, tiled=True)]
    all_to_all x1 -> x0, local copies, waits for them, and re-layouts: 2.29 us -> none  [body(): lax.all_to_all(query_proj, 'inner', split_axis=1, concat_axis=0, tiled=True)]
    another operation x0 -> x2, local copies, waits for them, and re-layouts: none -> 1.71 us  [the longest x1 1.57 us: keep_up_sources_all(): jnp.stack(jnp.split(original, axis_size('inner'), axis=join_dim), axis=0)]
  transfers between devices with their start and end apart: 2 -> 3, of which waited for: 0 -> 0; matrix products, arithmetic and copies ran while one was open for 4% -> 13% of each run, Pallas kernels for 0% -> 0%
where the time goes in v1:
time: 121 us
  blocking collectives  44.7 us (37%)
  local copies, waits for them, and re-layouts  23.8 us (20%)
  matrix products  17.6 us (15%)
  between operations  14.2 us (12%)
  other arithmetic  10.6 us (9%)
  starting transfers between devices  9.39 us (8%)
    all_to_all x1, blocking collectives, body(): lax.all_to_all(result, 'inner', split_axis=0, concat_axis=1, tiled=True)  17.8 us
    unnamed x16, local copies, waits for them, and re-layouts  15 us
    unnamed x1, blocking collectives  14.8 us
    all_gather x1, blocking collectives, body(): lax.all_gather(group_pos, 'outer', axis=0, tiled=True)  12.1 us
    dot_general x4, matrix products, update(): jnp.einsum('goi,ogt->git', softmax_weights.astype(jnp.bfloat16), value_sl...  11.9 us
    reduce_sum x4, other arithmetic, update(): running_sum = running_sum * rescale + jnp.sum(softmax_weights, axis=1)  8.73 us
    dot_general x4, matrix products, update(): jnp.einsum('lva,vga->vlg', key_slice, query_cluster, preferred_element_ty...  5.71 us
    all_to_all x1, starting transfers between devices, body(): lax.all_to_all(kv_spread, 'inner', split_axis=1, concat_axis=0, tiled=True)  5.2 us
  transfers between devices with their start and end apart: 3, of which 0 were waited for; matrix products, arithmetic and copies ran while one was open for 13% of the time, Pallas kernels for 0%

profile of v1, /device:TPU:0, one launch (start us, length us, event | category | flops | bytes accessed | tf_op | source)
XLA Modules:
  0.0 120.5 jit_solution(16819064252035802341)
XLA Ops:
  9.0 5.2 %all-to-all-start = ((bf16[64,8,256]{2,0,1:T(8,128)(2,1)}), bf16[64,8,256]{2,0,1:T(8,128)(2,1)S(1)}, u32[]{:S(2)}, u32[]{:S(2)}) async-start(bf16[64,8,256]{2,0,1:T(8,128)(2,1)} %pad_maximum_fusion), calls=%async_computation | async-start | bytes 524288 | tf_op jit(solution)/shard_map/all_to_all | solution.py:100
  14.3 1.6 %bitcast_dynamic-update-slice_fusion.7 = bf16[8,64,1024]{2,1,0:T(8,128)(2,1)} fusion(bf16[64,8192]{1,0:T(8,128)(2,1)} %param.6), kind=kLoop, calls=%fused_computation.38 | loop fusion | bytes 262144
  15.8 1.6 %bitcast_dynamic-update-slice_fusion.6 = bf16[8,64,1024]{2,1,0:T(8,128)(2,1)} fusion(bf16[8,64,1024]{2,1,0:T(8,128)(2,1)} %bitcast_dynamic-update-slice_fusion.7, bf16[64,8192]{1,0:T(8,128)(2,1)} %param.6), kind=kLoop, calls=%fused_computation.37 | loop fusion | bytes 262144
  17.4 1.6 %bitcast_dynamic-update-slice_fusion.5 = bf16[8,64,1024]{2,1,0:T(8,128)(2,1)} fusion(bf16[8,64,1024]{2,1,0:T(8,128)(2,1)} %bitcast_dynamic-update-slice_fusion.6, bf16[64,8192]{1,0:T(8,128)(2,1)} %param.6), kind=kLoop, calls=%fused_computation.36 | loop fusion | bytes 262144
  19.0 1.6 %bitcast_dynamic-update-slice_fusion.4 = bf16[8,64,1024]{2,1,0:T(8,128)(2,1)} fusion(bf16[8,64,1024]{2,1,0:T(8,128)(2,1)} %bitcast_dynamic-update-slice_fusion.5, bf16[64,8192]{1,0:T(8,128)(2,1)} %param.6), kind=kLoop, calls=%fused_computation.35 | loop fusion | bytes 262144
  20.5 1.6 %bitcast_dynamic-update-slice_fusion.3 = bf16[8,64,1024]{2,1,0:T(8,128)(2,1)} fusion(bf16[8,64,1024]{2,1,0:T(8,128)(2,1)} %bitcast_dynamic-update-slice_fusion.4, bf16[64,8192]{1,0:T(8,128)(2,1)} %param.6), kind=kLoop, calls=%fused_computation.34 | loop fusion | bytes 262144
  22.8 1.6 %bitcast_dynamic-update-slice_fusion.2 = bf16[8,64,1024]{2,1,0:T(8,128)(2,1)} fusion(bf16[8,64,1024]{2,1,0:T(8,128)(2,1)} %bitcast_dynamic-update-slice_fusion.3, bf16[64,8192]{1,0:T(8,128)(2,1)} %param.6), kind=kLoop, calls=%fused_computation.33 | loop fusion | bytes 262144
  24.4 1.6 %bitcast_dynamic-update-slice_fusion.1 = bf16[8,64,1024]{2,1,0:T(8,128)(2,1)} fusion(bf16[8,64,1024]{2,1,0:T(8,128)(2,1)} %bitcast_dynamic-update-slice_fusion.2, bf16[64,8192]{1,0:T(8,128)(2,1)} %param.6), kind=kLoop, calls=%fused_computation.32 | loop fusion | bytes 262144
  26.0 1.6 %bitcast_dynamic-update-slice_fusion = bf16[8,64,1024]{2,1,0:T(8,128)(2,1)} fusion(bf16[8,64,1024]{2,1,0:T(8,128)(2,1)} %bitcast_dynamic-update-slice_fusion.1, bf16[64,8192]{1,0:T(8,128)(2,1)} %param.6), kind=kLoop, calls=%fused_computation.31 | loop fusion | bytes 262144 | tf_op jit(solution)/shard_map/stack | solution.py:16
  27.5 4.2 %all-to-all-start.1 = ((bf16[8,64,1024]{2,1,0:T(8,128)(2,1)}), bf16[8,64,1024]{2,1,0:T(8,128)(2,1)S(1)}, u32[]{:S(2)}, u32[]{:S(2)}) async-start(bf16[8,64,1024]{2,1,0:T(8,128)(2,1)} %bitcast_dynamic-update-slice_fusion), calls=%async_computation.1 | async-start | bytes 2097152 | tf_op jit(solution)/shard_map/all_to_all | solution.py:15
  31.7 1.3 %dynamic-slice = u32[1]{0:T(128)} dynamic-slice(u32[32]{0:T(128)} %constant.26, u32[]{:T(128)S(6)} %add.9), dynamic_slice_sizes={1} | dynamic-slice | bytes 12
  34.5 14.8 %all-reduce = s32[512]{0:T(512)S(1)} all-reduce(s32[512]{0:T(512)S(1)} %dynamic-update-slice), channel_id=1, replica_groups=mesh['outer'=4,'inner'=8] {'inner'}, use_global_device_ids=true, to_apply=%add | all-reduce | flops 512 | bytes 4096
  49.3 12.1 %all-gather = s32[4,1,512]{2,1,0:T(1,128)S(1)} all-gather(s32[1,1,512]{2,1,0:T(1,128)S(1)} %bitcast.112), channel_id=1, replica_groups=mesh['outer'=4,'inner'=8] {'outer'}, dimensions={0}, use_global_device_ids=true | all-gather | bytes 10240 | tf_op jit(solution)/shard_map/all_gather | solution.py:116
  61.9 31.0 %while.15 = (s32[]{:T(128)}, f32[1,4096]{1,0:T(1,128)S(1)}, f32[1,4096]{1,0:T(1,128)S(1)}, f32[1,4096,128]{2,1,0:T(8,128)S(1)}, s32[4,512]{1,0:T(4,128)S(1)}, /*...) while((s32[]{:T(128)}, f32[1,4096]{1,0:T(1,128)S(1)}, ...), condition=%wide.region_3.4_spmd.clone, body=%wide.region_0.3_spmd.clone.sunk | while | flops 1104695296 | bytes 31568000 | solution.py:64
  62.0 1.0 dynamic-slice_bitcast_fusion.2
  63.0 1.4 %fusion.31 = (f32[4096]{0:T(1024)S(1)}, f32[512,4096]{1,0:T(8,128)S(1)}) fusion(s32[4096]{0:T(1024)S(1)} %bitcast.97, s32[512]{0:T(512)S(1)} %bitcast.109, bf16[1,4096,128]{2,1,0:T(8,128)(2,1)S(1)} %get-tuple-element.183, bf16[512,256]{1,0:T(8,128)(2,1)S(1)} %dynamic-slice_bitcast_fusion.2), kind=kOutput, calls=%fused_computation.3.clone.1 | convolution fusion | flops 545255424 | bytes 9603072 | tf_op jit(solution)/shard_map/while/body/eval_jaxpr/lva,vga->vlg/dot_general | solution.py:34
  64.4 2.2 %fusion.33 = f32[4096]{0:T(1024)S(1)} fusion(f32[512,4096]{1,0:T(8,128)S(1)} %get-tuple-element.154, f32[4096]{0:T(1024)S(1)} %bitcast.90, s32[4096]{0:T(1024)S(1)} %bitcast.98, s32[512]{0:T(512)S(1)} %bitcast.110), kind=kLoop, calls=%fused_computation.5.clone.1 | loop fusion | flops 10481664 | bytes 8439808 | tf_op jit(solution)/shard_map/while/body/eval_jaxpr/reduce_sum | solution.py:42
  66.7 3.0 %fusion.35 = f32[1,4096,128]{2,1,0:T(8,128)S(1)} fusion(f32[512,4096]{1,0:T(8,128)S(1)} %get-tuple-element.154, f32[4096]{0:T(1024)S(1)} %bitcast.91, s32[4096]{0:T(1024)S(1)} %bitcast.99, s32[512]{0:T(512)S(1)} %bitcast.111, f32[1,4096,128]{2,1,0:T(8,128)S(1)} %get-tuple-element.170, f32[4096]{0:T(1024)S(1)} %bitcast.108, pred[]{:T(512)S(6)} %compare.3, ...), kind=kOutput, calls=%fused_computation.7.clone.1 | convolution fusion | flops 548929536 | bytes 12765185 | tf_op jit(solution)/shard_map/while/body/eval_jaxpr/goi,ogt->git/dot_general | solution.py:43
  69.7 1.0 dynamic-slice_bitcast_fusion.2
  70.7 1.4 %fusion.31 = (f32[4096]{0:T(1024)S(1)}, f32[512,4096]{1,0:T(8,128)S(1)}) fusion(s32[4096]{0:T(1024)S(1)} %bitcast.97, s32[512]{0:T(512)S(1)} %bitcast.109, bf16[1,4096,128]{2,1,0:T(8,128)(2,1)S(1)} %get-tuple-element.183, bf16[512,256]{1,0:T(8,128)(2,1)S(1)} %dynamic-slice_bitcast_fusion.2), kind=kOutput, calls=%fused_computation.3.clone.1 | convolution fusion | flops 545255424 | bytes 9603072 | tf_op jit(solution)/shard_map/while/body/eval_jaxpr/lva,vga->vlg/dot_general | solution.py:34
  72.2 2.2 %fusion.33 = f32[4096]{0:T(1024)S(1)} fusion(f32[512,4096]{1,0:T(8,128)S(1)} %get-tuple-element.154, f32[4096]{0:T(1024)S(1)} %bitcast.90, s32[4096]{0:T(1024)S(1)} %bitcast.98, s32[512]{0:T(512)S(1)} %bitcast.110), kind=kLoop, calls=%fused_computation.5.clone.1 | loop fusion | flops 10481664 | bytes 8439808 | tf_op jit(solution)/shard_map/while/body/eval_jaxpr/reduce_sum | solution.py:42
  74.4 3.0 %fusion.35 = f32[1,4096,128]{2,1,0:T(8,128)S(1)} fusion(f32[512,4096]{1,0:T(8,128)S(1)} %get-tuple-element.154, f32[4096]{0:T(1024)S(1)} %bitcast.91, s32[4096]{0:T(1024)S(1)} %bitcast.99, s32[512]{0:T(512)S(1)} %bitcast.111, f32[1,4096,128]{2,1,0:T(8,128)S(1)} %get-tuple-element.170, f32[4096]{0:T(1024)S(1)} %bitcast.108, pred[]{:T(512)S(6)} %compare.3, ...), kind=kOutput, calls=%fused_computation.7.clone.1 | convolution fusion | flops 548929536 | bytes 12765185 | tf_op jit(solution)/shard_map/while/body/eval_jaxpr/goi,ogt->git/dot_general | solution.py:43
  77.5 1.0 dynamic-slice_bitcast_fusion.2
  78.5 1.4 %fusion.31 = (f32[4096]{0:T(1024)S(1)}, f32[512,4096]{1,0:T(8,128)S(1)}) fusion(s32[4096]{0:T(1024)S(1)} %bitcast.97, s32[512]{0:T(512)S(1)} %bitcast.109, bf16[1,4096,128]{2,1,0:T(8,128)(2,1)S(1)} %get-tuple-element.183, bf16[512,256]{1,0:T(8,128)(2,1)S(1)} %dynamic-slice_bitcast_fusion.2), kind=kOutput, calls=%fused_computation.3.clone.1 | convolution fusion | flops 545255424 | bytes 9603072 | tf_op jit(solution)/shard_map/while/body/eval_jaxpr/lva,vga->vlg/dot_general | solution.py:34
  79.9 2.2 %fusion.33 = f32[4096]{0:T(1024)S(1)} fusion(f32[512,4096]{1,0:T(8,128)S(1)} %get-tuple-element.154, f32[4096]{0:T(1024)S(1)} %bitcast.90, s32[4096]{0:T(1024)S(1)} %bitcast.98, s32[512]{0:T(512)S(1)} %bitcast.110), kind=kLoop, calls=%fused_computation.5.clone.1 | loop fusion | flops 10481664 | bytes 8439808 | tf_op jit(solution)/shard_map/while/body/eval_jaxpr/reduce_sum | solution.py:42
  82.2 3.0 %fusion.35 = f32[1,4096,128]{2,1,0:T(8,128)S(1)} fusion(f32[512,4096]{1,0:T(8,128)S(1)} %get-tuple-element.154, f32[4096]{0:T(1024)S(1)} %bitcast.91, s32[4096]{0:T(1024)S(1)} %bitcast.99, s32[512]{0:T(512)S(1)} %bitcast.111, f32[1,4096,128]{2,1,0:T(8,128)S(1)} %get-tuple-element.170, f32[4096]{0:T(1024)S(1)} %bitcast.108, pred[]{:T(512)S(6)} %compare.3, ...), kind=kOutput, calls=%fused_computation.7.clone.1 | convolution fusion | flops 548929536 | bytes 12765185 | tf_op jit(solution)/shard_map/while/body/eval_jaxpr/goi,ogt->git/dot_general | solution.py:43
  85.2 1.0 dynamic-slice_bitcast_fusion.2
  86.2 1.4 %fusion.31 = (f32[4096]{0:T(1024)S(1)}, f32[512,4096]{1,0:T(8,128)S(1)}) fusion(s32[4096]{0:T(1024)S(1)} %bitcast.97, s32[512]{0:T(512)S(1)} %bitcast.109, bf16[1,4096,128]{2,1,0:T(8,128)(2,1)S(1)} %get-tuple-element.183, bf16[512,256]{1,0:T(8,128)(2,1)S(1)} %dynamic-slice_bitcast_fusion.2), kind=kOutput, calls=%fused_computation.3.clone.1 | convolution fusion | flops 545255424 | bytes 9603072 | tf_op jit(solution)/shard_map/while/body/eval_jaxpr/lva,vga->vlg/dot_general | solution.py:34
  87.7 2.2 %fusion.33 = f32[4096]{0:T(1024)S(1)} fusion(f32[512,4096]{1,0:T(8,128)S(1)} %get-tuple-element.154, f32[4096]{0:T(1024)S(1)} %bitcast.90, s32[4096]{0:T(1024)S(1)} %bitcast.98, s32[512]{0:T(512)S(1)} %bitcast.110), kind=kLoop, calls=%fused_computation.5.clone.1 | loop fusion | flops 10481664 | bytes 8439808 | tf_op jit(solution)/shard_map/while/body/eval_jaxpr/reduce_sum | solution.py:42
  89.9 3.0 %fusion.35 = f32[1,4096,128]{2,1,0:T(8,128)S(1)} fusion(f32[512,4096]{1,0:T(8,128)S(1)} %get-tuple-element.154, f32[4096]{0:T(1024)S(1)} %bitcast.91, s32[4096]{0:T(1024)S(1)} %bitcast.99, s32[512]{0:T(512)S(1)} %bitcast.111, f32[1,4096,128]{2,1,0:T(8,128)S(1)} %get-tuple-element.170, f32[4096]{0:T(1024)S(1)} %bitcast.108, pred[]{:T(512)S(6)} %compare.3, ...), kind=kOutput, calls=%fused_computation.7.clone.1 | convolution fusion | flops 548929536 | bytes 12765185 | tf_op jit(solution)/shard_map/while/body/eval_jaxpr/goi,ogt->git/dot_general | solution.py:43
  94.8 17.8 %all_to_all.37 = bf16[8,64,1024]{2,1,0:T(8,128)(2,1)S(1)} all-to-all(bf16[8,64,1024]{2,1,0:T(8,128)(2,1)S(1)} %convert_element_type.20), channel_id=1, replica_groups=mesh['outer'=4,'inner'=8] {'inner'}, dimensions={0} | all-to-all | bytes 2097152 | tf_op jit(solution)/shard_map/all_to_all | solution.py:127
  112.6 1.1 copy.26
  (49 shorter events, 6.9 us)
Async XLA Ops:
  6.5 0.8 copy-start
  9.0 13.1 %all-to-all-start = ((bf16[64,8,256]{2,0,1:T(8,128)(2,1)}), bf16[64,8,256]{2,0,1:T(8,128)(2,1)S(1)}, u32[]{:S(2)}, u32[]{:S(2)}) async-start(bf16[64,8,256]{2,0,1:T(8,128)(2,1)} %pad_maximum_fusion), calls=%async_computation | async-start | bytes 524288 | tf_op jit(solution)/shard_map/all_to_all | solution.py:100
  14.2 47.7 %all-gather.3.cloned.1.call-start = ((), (), s32[]{:S(2)}) async-start(), calls=%async_computation.3 | async-start | bytes 1310720 | tf_op jit(solution)/shard_map/all_gather | solution.py:115
  22.1 0.7 copy-start.1
  27.5 33.9 %all-to-all-start.1 = ((bf16[8,64,1024]{2,1,0:T(8,128)(2,1)}), bf16[8,64,1024]{2,1,0:T(8,128)(2,1)S(1)}, u32[]{:S(2)}, u32[]{:S(2)}) async-start(bf16[8,64,1024]{2,1,0:T(8,128)(2,1)} %bitcast_dynamic-update-slice_fusion), calls=%async_computation.1 | async-start | bytes 2097152 | tf_op jit(solution)/shard_map/all_to_all | solution.py:15
Sparse Core Ops, SparseCore 0:
  23.0 29.6 all-gather.2
